TPU v7x, 1024 devices: a whole 4x4x32 slice. The times are simulated.
1024 devices in a mesh: grp: 128 (over y, z), tp: 4 (over x_lo, core), fs: 2 (over x_hi).
Axes of the slice: x: 4 (x_hi: 2, x_lo: 2; x = x_hi * 2 + x_lo), y: 4, z: 32, core: 2. Of those that a mesh axis runs over, the one named last changes fastest.
Arguments:
- tokens: bfloat16 [8192, 4, 8192], P('grp', None, ('tp', 'fs')), may hold values from -64 to 64
- norm_gain: bfloat16 [8192], P(('tp', 'fs')), may hold values from 0.25 to 1.75
- queries: bfloat16 [8192, 4, 8192], P('grp', None, ('tp', 'fs')), may hold values from -64 to 64
- rotated_key_cache: bfloat16 [8192, 32, 1024], P('grp', None, ('tp', 'fs')), may hold values from -6 to 6
- head_value_cache: bfloat16 [8192, 32, 1024], P('grp', None, ('tp', 'fs')), may hold values from -6 to 6
- lengths: int32 [8192], P('grp'), may hold values from 2 to 32
- master: float32 [8192, 2048], P('grp', ('tp', 'fs')), may hold values from -0.0625 to 0.0625
- moment_first: float32 [8192, 2048], P('grp', ('tp', 'fs')), may hold values from -4 to 4
- moment_second: float32 [8192, 2048], P('grp', ('tp', 'fs')), may hold values from 0.1 to 1
- gradient: float32 [8192, 2048], P('grp', ('tp', 'fs')), may hold values from -6 to 6
Outputs:
- attended: bfloat16 [8192, 4, 8192], P('grp', None, ('tp', 'fs'))
- appended: bfloat16 [8192, 4, 2048], P('grp', None, ('tp', 'fs'))
- new_master: float32 [8192, 2048], P('grp', ('tp', 'fs'))
- new_first: float32 [8192, 2048], P('grp', ('tp', 'fs'))
- new_second: float32 [8192, 2048], P('grp', ('tp', 'fs'))
All inputs are finite; a program needn't handle non-finite values.
Results may differ from a plain program's by a relative error of at most 0.0057.
Values may be sent and summed in bfloat16 or wider, within the bound.
No kernel may reach another device: no remote copies, remote signals or barrier semaphores. Data moves between devices by JAX's collectives and lax.ppermute only.
A program may use at most 64 MiB of HBM per device.

v0:
```python
import jax
import jax.numpy as jnp
from jax import lax
from jax.experimental import pallas as pl
from jax.experimental.pallas import tpu as pltpu
from jax.sharding import Mesh
from jax.sharding import PartitionSpec as P


MODEL_WIDTH = 8192
HEAD_SIZE = 128
GRP = ("y", "far", "near")
Z = ("far", "near")
COLS = ("xl", "c", "xh")


beta_first = 0.9
beta_second = 0.999
correct_first = 0.9999734386011124
correct_second = 0.09520785288629038
adam_eps = 1e-08
learn_rate = 0.003
decay_rate = 0.1
norm_eps = 1e-06
rope_base = 1000000.0

TOKENS = 256
EXTRA = 16
SLICE = 1024
CACHE_SLOTS = 32


def sums_block(sums):
    high = sums.astype(jnp.bfloat16).astype(jnp.float32)
    low = sums - high
    row = lax.broadcasted_iota(jnp.int32, (EXTRA, sums.shape[1]), 0)
    return jnp.where(row == 0, high, jnp.where(row == 1, low, 0.0)).astype(jnp.bfloat16)


def prepare_kernel(tokens_ref, gain_ref, out_ref):
    wide = tokens_ref[...].astype(jnp.float32)
    out_ref[:TOKENS, :] = (wide * gain_ref[...].astype(jnp.float32)).astype(jnp.bfloat16)
    sums = jnp.sum(wide * wide, axis=1, keepdims=True)
    sums = jnp.transpose(jnp.broadcast_to(sums, (TOKENS, 128)))[:1, :]
    out_ref[TOKENS:, :TOKENS] = sums_block(sums)
    out_ref[TOKENS:, TOKENS:] = jnp.zeros((EXTRA, SLICE - TOKENS), jnp.bfloat16)


def prepare(tokens, gain):
    return pl.pallas_call(
        prepare_kernel,
        out_shape=jax.ShapeDtypeStruct((TOKENS + EXTRA, SLICE), jnp.bfloat16),
        compiler_params=pltpu.CompilerParams(vmem_limit_bytes=8 << 20),
        name="prepare",
    )(tokens, gain)


def join_kernel(*refs):
    *parts, out_ref = refs
    for k, part in enumerate(parts):
        out_ref[256 * k : 256 * (k + 1), :] = part[...]


def joined(*parts):
    return pl.pallas_call(
        join_kernel,
        out_shape=jax.ShapeDtypeStruct((256 * len(parts), 256), jnp.bfloat16),
        compiler_params=pltpu.CompilerParams(vmem_limit_bytes=2 << 20),
        name="joined",
    )(*parts)


def project_kernel(own_ref, other_ref, *refs):
    w_refs, out_ref, layer = refs[:3], refs[3], refs[4]
    near, core = lax.axis_index("near"), lax.axis_index("c")
    x = lax.axis_index("xh") * 2 + lax.axis_index("xl")
    for w_ref, offsets in zip(w_refs, ((0, 5, 3), (7, 4, 2), (1, 6, 4))):
        for k, offset in enumerate(offsets):
            place = lax.rem(near + offset, 8)
            layer[:, :, place] = w_ref[256 * k : 256 * (k + 1), :].reshape(2, 2, 64, 256)
    for a_ref, c in ((own_ref, core), (other_ref, 1 - core)):
        for low in range(2):
            slots = [lax.rem(x + 4 - (2 * high + low), 4) for high in range(2)]
            total = jnp.zeros((TOKENS, 256), jnp.float32)
            sums = jnp.zeros((1, TOKENS), jnp.float32)
            for high, slot in enumerate(slots):
                total += jnp.dot(
                    a_ref[slot, :TOKENS, :],
                    layer[high].reshape(SLICE, 256),
                    preferred_element_type=jnp.float32,
                )
                tail = a_ref[slot, TOKENS:, :TOKENS].astype(jnp.float32)
                sums += tail[0:1] + tail[1:2]
            out_ref[2 * low + c, :TOKENS, :] = total.astype(jnp.bfloat16)
            out_ref[2 * low + c, TOKENS:, :] = sums_block(sums)


def project(own, other, blocks):
    return pl.pallas_call(
        project_kernel,
        out_shape=jax.ShapeDtypeStruct((4, TOKENS + EXTRA, 256), jnp.bfloat16),
        scratch_shapes=[pltpu.VMEM((2, 2, 8, 64, 256), jnp.bfloat16)],
        compiler_params=pltpu.CompilerParams(vmem_limit_bytes=16 << 20),
        name="project",
    )(own, other, *blocks)


def group_queries(queries_ref, group):
    at = pl.ds(16 * group, 16)
    return jnp.concatenate(
        [queries_ref[at, pl.ds(HEAD_SIZE * head, HEAD_SIZE)] for head in range(8)], axis=0
    )


def cached_kernel(lengths_ref, queries_ref, keys_ref, values_ref, sums_ref, stats_ref):
    row = lax.broadcasted_iota(jnp.int32, (128, 128), 0)
    lane = lax.broadcasted_iota(jnp.int32, (128, 128), 1)
    same_row = (row // 4) % 4 == lane // CACHE_SLOTS
    for group in range(16):
        at = pl.ds(128 * group, 128)
        longest = jnp.zeros((128, 128), jnp.int32)
        for k in range(4):
            longest = jnp.where(lane // CACHE_SLOTS == k, lengths_ref[4 * group + k], longest)
        scores = lax.dot_general(
            group_queries(queries_ref, group),
            keys_ref[at, :],
            (((1,), (1,)), ((), ())),
            preferred_element_type=jnp.float32,
        ) * (HEAD_SIZE**-0.5)
        scores = jnp.where(same_row & (lane % CACHE_SLOTS < longest), scores, -jnp.inf)
        top = jnp.max(scores, axis=1, keepdims=True)
        probs = jnp.exp(scores - top)
        total = jnp.sum(probs, axis=1, keepdims=True)
        sums_ref[at, :] = jnp.dot(
            probs.astype(jnp.bfloat16), values_ref[at, :], preferred_element_type=jnp.float32
        )
        stats_ref[:, group : group + 1] = top
        stats_ref[:, 16 + group : 17 + group] = total


def cached_part(lengths, queries, keys, values):
    vmem = pl.BlockSpec(memory_space=pltpu.VMEM)
    return pl.pallas_call(
        cached_kernel,
        in_specs=[pl.BlockSpec(memory_space=pltpu.SMEM), vmem, vmem, vmem],
        out_shape=[
            jax.ShapeDtypeStruct((2048, HEAD_SIZE), jnp.float32),
            jax.ShapeDtypeStruct((128, 128), jnp.float32),
        ],
        compiler_params=pltpu.CompilerParams(vmem_limit_bytes=12 << 20),
        cost_estimate=pl.CostEstimate(flops=150_000_000, bytes_accessed=3 << 20, transcendentals=1 << 18),
        name="cached",
    )(lengths, queries, keys, values)


def finish_kernel(
    parts_ref, cosine_ref, sine_ref, queries_ref, sums_ref, stats_ref, attended_ref, appended_ref
):
    total = jnp.zeros((TOKENS, 256), jnp.float32)
    sums = jnp.zeros((1, TOKENS), jnp.float32)
    for k in range(4):
        total += parts_ref[k, :TOKENS, :].astype(jnp.float32)
        tail = parts_ref[k, TOKENS:, :].astype(jnp.float32)
        sums += tail[0:1] + tail[1:2]
    scale = lax.rsqrt(sums / MODEL_WIDTH + norm_eps)
    scale = jnp.transpose(jnp.broadcast_to(scale, (HEAD_SIZE, TOKENS)))
    keys = total[:, :HEAD_SIZE] * scale
    keys = keys * cosine_ref[...] + pltpu.roll(keys, HEAD_SIZE // 2, 1) * sine_ref[...]
    keys = keys.astype(jnp.bfloat16)
    values = (total[:, HEAD_SIZE:] * scale).astype(jnp.bfloat16)
    appended_ref[:, :, :HEAD_SIZE] = keys.reshape(64, 4, HEAD_SIZE)
    appended_ref[:, :, HEAD_SIZE:] = values.reshape(64, 4, HEAD_SIZE)
    row = lax.broadcasted_iota(jnp.int32, (128, 16), 0)
    lane = lax.broadcasted_iota(jnp.int32, (128, 16), 1)
    seen = ((row // 4) % 4 == lane // 4) & (lane % 4 <= row % 4)
    for group in range(16):
        at = pl.ds(128 * group, 128)
        near = slice(16 * group, 16 * group + 16)
        scores = lax.dot_general(
            group_queries(queries_ref, group),
            keys[near],
            (((1,), (1,)), ((), ())),
            preferred_element_type=jnp.float32,
        ) * (HEAD_SIZE**-0.5)
        scores = jnp.where(seen, scores, -jnp.inf)
        old_top = stats_ref[:, group : group + 1]
        old_total = stats_ref[:, 16 + group : 17 + group]
        top = jnp.maximum(jnp.max(scores, axis=1, keepdims=True), old_top)
        probs = jnp.exp(scores - top)
        factor = jnp.exp(old_top - top)
        denom = jnp.sum(probs, axis=1, keepdims=True) + old_total * factor
        blended = sums_ref[at, :] * factor + jnp.dot(
            probs.astype(jnp.bfloat16), values[near], preferred_element_type=jnp.float32
        )
        blended = (blended / denom).astype(jnp.bfloat16)
        for head in range(8):
            attended_ref[4 * group : 4 * group + 4, :, HEAD_SIZE * head : HEAD_SIZE * (head + 1)] = (
                blended[16 * head : 16 * head + 16].reshape(4, 4, HEAD_SIZE)
            )


def finish(parts, cosine, sine, queries, sums, stats):
    return pl.pallas_call(
        finish_kernel,
        out_shape=[
            jax.ShapeDtypeStruct((TOKENS // 4, 4, SLICE), jnp.bfloat16),
            jax.ShapeDtypeStruct((TOKENS // 4, 4, 256), jnp.bfloat16),
        ],
        compiler_params=pltpu.CompilerParams(vmem_limit_bytes=12 << 20),
        name="finish",
    )(parts, cosine, sine, queries, sums, stats)


def turns(lengths, steps):
    half = HEAD_SIZE // 2
    frequency = rope_base ** (-(jnp.arange(half, dtype=jnp.float32) * 2.0 / HEAD_SIZE))
    positions = (lengths[:, None] + jnp.arange(steps, dtype=jnp.int32)[None, :]).astype(jnp.float32)
    angles = positions.reshape(-1)[:, None] * frequency[None, :]
    cosine, sine = jnp.cos(angles), jnp.sin(angles)
    return jnp.concatenate([cosine, cosine], axis=1), jnp.concatenate([-sine, sine], axis=1)


def along_x(array, shift):
    at = [(x % 2) * 2 + x // 2 for x in range(4)]
    return lax.ppermute(array, ("xl", "xh"), [(at[x], at[(x + shift) % 4]) for x in range(4)])


def along_z(array, shift):
    return lax.ppermute(array, Z, [(z, (z + shift) % 32) for z in range(32)])


def shards(
    tokens,
    norm_gain,
    queries,
    rotated_key_cache,
    head_value_cache,
    lengths,
    master,
    moment_first,
    moment_second,
    gradient,
):
    batch_rows, steps = (tokens.shape[0], tokens.shape[1])
    exchange = [(a * 4 + b, b * 4 + a) for a in range(4) for b in range(4)]
    turned = lax.ppermute(tokens, ("y", "xl", "c"), exchange)
    gain = lax.ppermute(norm_gain.reshape(1, SLICE), ("y", "xl", "c"), exchange)
    turned = prepare(turned.reshape(TOKENS, SLICE), gain)
    average = beta_first * moment_first + (1.0 - beta_first) * gradient
    variance = beta_second * moment_second + (1.0 - beta_second) * gradient * gradient
    update = average / correct_first / (jnp.sqrt(variance / correct_second) + adam_eps)
    renewed = master - learn_rate * (update + decay_rate * master)
    layer_half = renewed.astype(jnp.bfloat16)
    columns = layer_half.shape[1]
    spread = lax.all_to_all(jnp.broadcast_to(layer_half[None], (4, 64, columns)), "far", 0, 0)
    spread = spread.reshape(256, columns)
    ring = []
    for d in (2, 1, 3):
        ring.append(along_x(turned, d))
    own = jnp.stack([turned, ring[1], ring[0], ring[2]])
    other = lax.ppermute(own, "c", [(0, 1), (1, 0)])
    below = along_z(spread, 3)
    above = along_z(spread, 29)
    held = joined(spread, below, above)
    from_below = along_z(held, 1)
    from_above = along_z(held, 31)
    queries_flat = queries.reshape(TOKENS, SLICE)
    old_sums, old_stats = cached_part(
        lengths,
        queries_flat,
        rotated_key_cache.reshape(batch_rows * CACHE_SLOTS, HEAD_SIZE),
        head_value_cache.reshape(batch_rows * CACHE_SLOTS, HEAD_SIZE),
    )
    cosine, sine = turns(lengths, steps)
    partial = project(own, other, [held, from_below, from_above])
    parts = lax.all_to_all(partial, "y", 0, 0)
    attended, appended = finish(parts, cosine, sine, queries_flat, old_sums, old_stats)
    return (
        attended,
        appended,
        renewed,
        average,
        variance,
    )


def solution(mesh):
    split = Mesh(
        mesh.devices.reshape(4, 4, 8, 2, 2, 2),
        ("y", "far", "near", "xl", "c", "xh"),
    )
    placed = (
        P(GRP, None, COLS),
        P(COLS),
        P(GRP, None, COLS),
        P(GRP, None, COLS),
        P(GRP, None, COLS),
        P(GRP),
        P(GRP, COLS),
        P(GRP, COLS),
        P(GRP, COLS),
        P(GRP, COLS),
    )
    return jax.shard_map(
        shards,
        mesh=split,
        in_specs=placed,
        out_specs=(
            P(GRP, None, COLS),
            P(GRP, None, COLS),
            P(GRP, COLS),
            P(GRP, COLS),
            P(GRP, COLS),
        ),
        check_vma=False,
    )
```

profile of v0, /device:TPU:34, one launch (start us, length us, event | category | flops | bytes accessed | tf_op | source)
XLA Modules:
  0.0 168.7 jit_solution(529622231197880280)
XLA Ops:
  0.6 5.1 %collective-permute-start = (bf16[64,4,1024]{2,1,0:T(4,128)(2,1)}, bf16[64,4,1024]{2,1,0:T(4,128)(2,1)S(1)}, u32[]{:S(2)}, u32[]{:S(2)}) collective-permute-start(bf16[64,4,1024]{2,1,0:T(4,128)(2,1)} %param.10), channel_id=1, source_target_pairs={{0,0},{2,256},{4,512},{6,768},{256,2},{258,258},{260,514},{262,770... | collective-permute-start | bytes 1572872 | tf_op jit(solution)/shard_map/ppermute | solution.py:246
  5.7 0.7 reshape.53
  6.4 3.2 %collective-permute-start.1 = (bf16[1,1024]{1,0:T(2,128)(2,1)S(1)}, bf16[1,1024]{1,0:T(2,128)(2,1)S(1)}, u32[]{:S(2)}, u32[]{:S(2)}) collective-permute-start(bf16[1,1024]{1,0:T(2,128)(2,1)S(1)} %reshape.53), channel_id=1, source_target_pairs={{0,0},{2,256},{4,512},{6,768},{256,2},{258,258},{260,514},{262,770... | collective-permute-start | bytes 6152 | tf_op jit(solution)/shard_map/ppermute | solution.py:247
  9.6 10.0 %collective-permute-done = bf16[64,4,1024]{2,1,0:T(4,128)(2,1)S(1)} collective-permute-done((bf16[64,4,1024]{2,1,0:T(4,128)(2,1)}, bf16[64,4,1024]{2,1,0:T(4,128)(2,1)S(1)}, u32[]{:S(2)}, u32[]{:S(2)}) %collective-permute-start) | collective-permute-done | bytes 524320 | tf_op jit(solution)/shard_map/ppermute | solution.py:246
  19.5 0.1 reshape.52.tokens_ref
  19.6 0.0 collective-permute-done.1.gain_ref
  19.7 0.3 prepare.1
  19.9 1.9 %collective-permute-start.2 = (bf16[272,1024]{1,0:T(8,128)(2,1)S(1)}, bf16[272,1024]{1,0:T(8,128)(2,1)S(1)}, u32[]{:S(2)}, u32[]{:S(2)}) collective-permute-start(bf16[272,1024]{1,0:T(8,128)(2,1)S(1)} %prepare.1), channel_id=1, source_target_pairs={{0,4},{4,1},{1,5},{5,0},{2,6},{6,3},{3,7},{7,2},{8,12},{12,9},{9,1... | collective-permute-start | bytes 1671176 | tf_op jit(solution)/shard_map/ppermute | solution.py:225
  21.8 4.0 %collective-permute-start.3 = (bf16[272,1024]{1,0:T(8,128)(2,1)S(1)}, bf16[272,1024]{1,0:T(8,128)(2,1)S(1)}, u32[]{:S(2)}, u32[]{:S(2)}) collective-permute-start(bf16[272,1024]{1,0:T(8,128)(2,1)S(1)} %prepare.1), channel_id=1, source_target_pairs={{0,1},{4,5},{1,0},{5,4},{2,3},{6,7},{3,2},{7,6},{8,9},{12,13},{9,8... | collective-permute-start | bytes 1671176 | tf_op jit(solution)/shard_map/ppermute | solution.py:225
  25.9 4.5 %collective-permute-start.4 = (bf16[272,1024]{1,0:T(8,128)(2,1)S(1)}, bf16[272,1024]{1,0:T(8,128)(2,1)S(1)}, u32[]{:S(2)}, u32[]{:S(2)}) collective-permute-start(bf16[272,1024]{1,0:T(8,128)(2,1)S(1)} %prepare.1), channel_id=1, source_target_pairs={{0,5},{4,0},{1,4},{5,1},{2,7},{6,2},{3,6},{7,3},{8,13},{12,8},{9,1... | collective-permute-start | bytes 1671176 | tf_op jit(solution)/shard_map/ppermute | solution.py:225
  30.4 6.9 %collective-permute-done.2 = bf16[272,1024]{1,0:T(8,128)(2,1)S(1)} collective-permute-done((bf16[272,1024]{1,0:T(8,128)(2,1)S(1)}, bf16[272,1024]{1,0:T(8,128)(2,1)S(1)}, u32[]{:S(2)}, u32[]{:S(2)}) %collective-permute-start.2) | collective-permute-done | bytes 557088 | tf_op jit(solution)/shard_map/ppermute | solution.py:225
  37.3 3.5 %collective-permute-done.3 = bf16[272,1024]{1,0:T(8,128)(2,1)S(1)} collective-permute-done((bf16[272,1024]{1,0:T(8,128)(2,1)S(1)}, bf16[272,1024]{1,0:T(8,128)(2,1)S(1)}, u32[]{:S(2)}, u32[]{:S(2)}) %collective-permute-start.3) | collective-permute-done | bytes 557088 | tf_op jit(solution)/shard_map/ppermute | solution.py:225
  40.8 10.2 %collective-permute-done.4 = bf16[272,1024]{1,0:T(8,128)(2,1)S(1)} collective-permute-done((bf16[272,1024]{1,0:T(8,128)(2,1)S(1)}, bf16[272,1024]{1,0:T(8,128)(2,1)S(1)}, u32[]{:S(2)}, u32[]{:S(2)}) %collective-permute-start.4) | collective-permute-done | bytes 557088 | tf_op jit(solution)/shard_map/ppermute | solution.py:225
  51.0 0.0 copy-start.6
  51.0 0.3 pad_maximum_fusion.own_ref
  51.3 1.9 %collective-permute-start.5 = (bf16[4,272,1024]{2,1,0:T(8,128)(2,1)S(1)}, bf16[4,272,1024]{2,1,0:T(8,128)(2,1)}, u32[]{:S(2)}, u32[]{:S(2)}) collective-permute-start(bf16[4,272,1024]{2,1,0:T(8,128)(2,1)S(1)} %pad_maximum_fusion.own_ref), channel_id=1, source_target_pairs={{0,2},{2,0},{1,3},{3,1},{4,6},{6,4},{5,7},{7,5},{8,10},{10,8},{9,1... | collective-permute-start | bytes 6684680 | tf_op jit(solution)/shard_map/ppermute | solution.py:261
  53.2 0.0 copy-done.7
  53.2 0.0 copy-done.8
  53.2 0.0 copy-done.9
  53.2 0.0 copy-done.10
  53.2 0.7 fusion.2
  54.0 58.9 %all_to_all.10 = bf16[4,64,256]{2,1,0:T(8,128)(2,1)S(1)} all-to-all(bf16[4,64,256]{2,1,0:T(8,128)(2,1)S(1)} %broadcast_in_dim.2), channel_id=1, replica_groups=mesh['y'=4,'far'=4,'near'=8,'xl'=2,'c'=2,'xh'=2] {'far'}, dimensions={0} | all-to-all | bytes 262144 | tf_op jit(solution)/shard_map/all_to_all | solution.py:255
  112.9 5.1 %collective-permute-start.6 = (bf16[256,256]{1,0:T(8,128)(2,1)S(1)}, bf16[256,256]{1,0:T(8,128)(2,1)S(1)}, u32[]{:S(2)}, u32[]{:S(2)}) collective-permute-start(bf16[256,256]{1,0:T(8,128)(2,1)S(1)} %bitcast.10), channel_id=1, source_target_pairs={{0,24},{8,32},{16,40},{24,48},{32,56},{40,64},{48,72},{56,80},{64,... | collective-permute-start | bytes 393224 | tf_op jit(solution)/shard_map/ppermute | solution.py:229
  118.0 3.8 %collective-permute-start.7 = (bf16[256,256]{1,0:T(8,128)(2,1)S(1)}, bf16[256,256]{1,0:T(8,128)(2,1)S(1)}, u32[]{:S(2)}, u32[]{:S(2)}) collective-permute-start(bf16[256,256]{1,0:T(8,128)(2,1)S(1)} %bitcast.11), channel_id=1, source_target_pairs={{0,232},{8,240},{16,248},{24,0},{32,8},{40,16},{48,24},{56,32},{64... | collective-permute-start | bytes 393224 | tf_op jit(solution)/shard_map/ppermute | solution.py:229
  121.7 1.0 collective-permute-done.6.refs_1_
  122.7 6.2 %collective-permute-done.7.refs_2_ = bf16[256,256]{1,0:T(8,128)(2,1)S(1)} collective-permute-done((bf16[256,256]{1,0:T(8,128)(2,1)S(1)}, bf16[256,256]{1,0:T(8,128)(2,1)S(1)}, u32[]{:S(2)}, u32[]{:S(2)}) %collective-permute-start.7) | collective-permute-done | bytes 131104 | tf_op jit(solution)/shard_map/ppermute | solution.py:229
  129.0 1.9 %collective-permute-start.8 = (bf16[768,256]{1,0:T(8,128)(2,1)S(1)}, bf16[768,256]{1,0:T(8,128)(2,1)S(1)}, u32[]{:S(2)}, u32[]{:S(2)}) collective-permute-start(bf16[768,256]{1,0:T(8,128)(2,1)S(1)} %joined.1.refs_0_), channel_id=1, source_target_pairs={{0,8},{8,16},{16,24},{24,32},{32,40},{40,48},{48,56},{56,64},{64,7... | collective-permute-start | bytes 1179656 | tf_op jit(solution)/shard_map/ppermute | solution.py:229
  130.9 3.9 %collective-permute-start.9 = (bf16[768,256]{1,0:T(8,128)(2,1)S(1)}, bf16[768,256]{1,0:T(8,128)(2,1)}, u32[]{:S(2)}, u32[]{:S(2)}) collective-permute-start(bf16[768,256]{1,0:T(8,128)(2,1)S(1)} %joined.1.refs_0_), channel_id=1, source_target_pairs={{0,248},{8,0},{16,8},{24,16},{32,24},{40,32},{48,40},{56,48},{64,5... | collective-permute-start | bytes 1179656 | tf_op jit(solution)/shard_map/ppermute | solution.py:229
  134.8 0.1 add_convert_fusion
  134.9 0.1 convert_element_type.15
  135.0 1.2 reshape.55.queries_ref
  136.2 0.0 copy-start.2
  136.2 1.0 copy-done.2
  137.2 1.0 copy-done.3
  138.3 4.5 %cached.1 = (f32[2048,128]{1,0:T(8,128)S(1)}, f32[128,128]{1,0:T(8,128)S(1)}) custom-call(s32[64]{0:T(128)S(1)} %copy-done.6, bf16[256,1024]{1,0:T(8,128)(2,1)S(1)} %reshape.55.queries_ref, bf16[2048,128]{1,0:T(8,128)(2,1)S(1)} %bitcast.8, bf16[2048,128]{1,0:T(8,128)(2,1)S(1)} %bitcast.9), custom_call_target="tpu_custom_call" | custom-call | flops 150000000 | bytes 3145728 | tf_op jit(solution)/shard_map/cached/pallas_call | solution.py:143
  142.7 0.0 copy-start
  142.8 1.0 copy-done
  143.7 0.6 copy-done.4
  144.4 0.0 collective-permute-done.8.refs_1_
  144.4 0.0 collective-permute-done.9.refs_2_
  144.4 0.0 collective-permute-done.5.other_ref
  144.4 3.8 %project.1 = bf16[4,272,256]{2,1,0:T(8,128)(2,1)} custom-call(bf16[4,272,1024]{2,1,0:T(8,128)(2,1)S(1)} %pad_maximum_fusion.own_ref, bf16[4,272,1024]{2,1,0:T(8,128)(2,1)} %collective-permute-done.5.other_ref, bf16[768,256]{1,0:T(8,128)(2,1)S(1)} %joined.1.refs_0_, bf16[768,256]{1,0:T(8,128)(2,1)S(1)} %collective-permute-done.8.refs_1_, ...), custom_call_target="tpu_custom_call" | custom-call | tf_op jit(solution)/shard_map/project/pallas_call | solution.py:99
  148.2 5.7 %all-to-all-start.1 = ((bf16[4,272,256]{2,1,0:T(8,128)(2,1)}), bf16[4,272,256]{2,1,0:T(8,128)(2,1)S(1)}, u32[]{:S(2)}, u32[]{:S(2)}) async-start(bf16[4,272,256]{2,1,0:T(8,128)(2,1)} %project.1), calls=%async_computation.1 | async-start | bytes 1114112 | tf_op jit(solution)/shard_map/all_to_all | solution.py:276
  153.9 0.5 fusion.1
  154.4 0.1 pad_maximum_fusion.1
  154.6 7.6 %all-to-all-done.1.parts_ref = bf16[4,272,256]{2,1,0:T(8,128)(2,1)S(1)} async-done(((bf16[4,272,256]{2,1,0:T(8,128)(2,1)}), bf16[4,272,256]{2,1,0:T(8,128)(2,1)S(1)}, u32[]{:S(2)}, u32[]{:S(2)}) %all-to-all-start.1) | async-done | bytes 557088 | tf_op jit(solution)/shard_map/all_to_all | solution.py:276
  162.1 0.8 copy-done.5
  163.0 5.8 %finish.1 = (bf16[64,4,1024]{2,1,0:T(4,128)(2,1)}, bf16[64,4,256]{2,1,0:T(4,128)(2,1)}) custom-call(bf16[4,272,256]{2,1,0:T(8,128)(2,1)S(1)} %all-to-all-done.1.parts_ref, f32[256,128]{1,0:T(8,128)S(1)} %get-tuple-element.20.cosine_ref, f32[256,128]{1,0:T(8,128)S(1)} %get-tuple-element.21.sine_ref, bf16[256,1024]{1,0:T(8,128)(2,1)S(1)} %reshape.55.queries_ref, ...), custom_call_target="tpu_custom_call" | custom-call | tf_op jit(solution)/shard_map/finish/pallas_call | solution.py:203
  (13 shorter events, 0.1 us)
Async XLA Ops:
  0.6 18.9 %collective-permute-start = (bf16[64,4,1024]{2,1,0:T(4,128)(2,1)}, bf16[64,4,1024]{2,1,0:T(4,128)(2,1)S(1)}, u32[]{:S(2)}, u32[]{:S(2)}) collective-permute-start(bf16[64,4,1024]{2,1,0:T(4,128)(2,1)} %param.10), channel_id=1, source_target_pairs={{0,0},{2,256},{4,512},{6,768},{256,2},{258,258},{260,514},{262,770... | collective-permute-start | bytes 1572872 | tf_op jit(solution)/shard_map/ppermute | solution.py:246
  6.4 13.2 %collective-permute-start.1 = (bf16[1,1024]{1,0:T(2,128)(2,1)S(1)}, bf16[1,1024]{1,0:T(2,128)(2,1)S(1)}, u32[]{:S(2)}, u32[]{:S(2)}) collective-permute-start(bf16[1,1024]{1,0:T(2,128)(2,1)S(1)} %reshape.53), channel_id=1, source_target_pairs={{0,0},{2,256},{4,512},{6,768},{256,2},{258,258},{260,514},{262,770... | collective-permute-start | bytes 6152 | tf_op jit(solution)/shard_map/ppermute | solution.py:247
  19.9 17.4 %collective-permute-start.2 = (bf16[272,1024]{1,0:T(8,128)(2,1)S(1)}, bf16[272,1024]{1,0:T(8,128)(2,1)S(1)}, u32[]{:S(2)}, u32[]{:S(2)}) collective-permute-start(bf16[272,1024]{1,0:T(8,128)(2,1)S(1)} %prepare.1), channel_id=1, source_target_pairs={{0,4},{4,1},{1,5},{5,0},{2,6},{6,3},{3,7},{7,2},{8,12},{12,9},{9,1... | collective-permute-start | bytes 1671176 | tf_op jit(solution)/shard_map/ppermute | solution.py:225
  21.8 18.9 %collective-permute-start.3 = (bf16[272,1024]{1,0:T(8,128)(2,1)S(1)}, bf16[272,1024]{1,0:T(8,128)(2,1)S(1)}, u32[]{:S(2)}, u32[]{:S(2)}) collective-permute-start(bf16[272,1024]{1,0:T(8,128)(2,1)S(1)} %prepare.1), channel_id=1, source_target_pairs={{0,1},{4,5},{1,0},{5,4},{2,3},{6,7},{3,2},{7,6},{8,9},{12,13},{9,8... | collective-permute-start | bytes 1671176 | tf_op jit(solution)/shard_map/ppermute | solution.py:225
  25.9 25.1 %collective-permute-start.4 = (bf16[272,1024]{1,0:T(8,128)(2,1)S(1)}, bf16[272,1024]{1,0:T(8,128)(2,1)S(1)}, u32[]{:S(2)}, u32[]{:S(2)}) collective-permute-start(bf16[272,1024]{1,0:T(8,128)(2,1)S(1)} %prepare.1), channel_id=1, source_target_pairs={{0,5},{4,0},{1,4},{5,1},{2,7},{6,2},{3,6},{7,3},{8,13},{12,8},{9,1... | collective-permute-start | bytes 1671176 | tf_op jit(solution)/shard_map/ppermute | solution.py:225
  51.0 2.2 %copy-start.7 = (f32[64,256]{1,0:T(8,128)S(1)}, f32[64,256]{1,0:T(8,128)}, u32[]{:S(2)}) copy-start(f32[64,256]{1,0:T(8,128)} %param.16) | copy-start | bytes 196612
  51.0 2.3 %copy-start.8 = (f32[64,256]{1,0:T(8,128)S(1)}, f32[64,256]{1,0:T(8,128)}, u32[]{:S(2)}) copy-start(f32[64,256]{1,0:T(8,128)} %param.19) | copy-start | bytes 196612
  51.0 2.3 %copy-start.9 = (f32[64,256]{1,0:T(8,128)S(1)}, f32[64,256]{1,0:T(8,128)}, u32[]{:S(2)}) copy-start(f32[64,256]{1,0:T(8,128)} %param.17) | copy-start | bytes 196612
  51.0 2.3 %copy-start.10 = (f32[64,256]{1,0:T(8,128)S(1)}, f32[64,256]{1,0:T(8,128)}, u32[]{:S(2)}) copy-start(f32[64,256]{1,0:T(8,128)} %param.18) | copy-start | bytes 196612
  51.0 83.8 %copy-start.6 = (s32[64]{0:T(128)S(1)}, s32[64]{0:T(128)}, u32[]{:S(2)}) copy-start(s32[64]{0:T(128)} %lengths_ref.1) | copy-start | bytes 772
  51.3 93.1 %collective-permute-start.5 = (bf16[4,272,1024]{2,1,0:T(8,128)(2,1)S(1)}, bf16[4,272,1024]{2,1,0:T(8,128)(2,1)}, u32[]{:S(2)}, u32[]{:S(2)}) collective-permute-start(bf16[4,272,1024]{2,1,0:T(8,128)(2,1)S(1)} %pad_maximum_fusion.own_ref), channel_id=1, source_target_pairs={{0,2},{2,0},{1,3},{3,1},{4,6},{6,4},{5,7},{7,5},{8,10},{10,8},{9,1... | collective-permute-start | bytes 6684680 | tf_op jit(solution)/shard_map/ppermute | solution.py:261
  112.9 9.9 %collective-permute-start.6 = (bf16[256,256]{1,0:T(8,128)(2,1)S(1)}, bf16[256,256]{1,0:T(8,128)(2,1)S(1)}, u32[]{:S(2)}, u32[]{:S(2)}) collective-permute-start(bf16[256,256]{1,0:T(8,128)(2,1)S(1)} %bitcast.10), channel_id=1, source_target_pairs={{0,24},{8,32},{16,40},{24,48},{32,56},{40,64},{48,72},{56,80},{64,... | collective-permute-start | bytes 393224 | tf_op jit(solution)/shard_map/ppermute | solution.py:229
  118.0 11.0 %collective-permute-start.7 = (bf16[256,256]{1,0:T(8,128)(2,1)S(1)}, bf16[256,256]{1,0:T(8,128)(2,1)S(1)}, u32[]{:S(2)}, u32[]{:S(2)}) collective-permute-start(bf16[256,256]{1,0:T(8,128)(2,1)S(1)} %bitcast.11), channel_id=1, source_target_pairs={{0,232},{8,240},{16,248},{24,0},{32,8},{40,16},{48,24},{56,32},{64... | collective-permute-start | bytes 393224 | tf_op jit(solution)/shard_map/ppermute | solution.py:229
  129.0 15.4 %collective-permute-start.8 = (bf16[768,256]{1,0:T(8,128)(2,1)S(1)}, bf16[768,256]{1,0:T(8,128)(2,1)S(1)}, u32[]{:S(2)}, u32[]{:S(2)}) collective-permute-start(bf16[768,256]{1,0:T(8,128)(2,1)S(1)} %joined.1.refs_0_), channel_id=1, source_target_pairs={{0,8},{8,16},{16,24},{24,32},{32,40},{40,48},{48,56},{56,64},{64,7... | collective-permute-start | bytes 1179656 | tf_op jit(solution)/shard_map/ppermute | solution.py:229
  130.9 13.5 %collective-permute-start.9 = (bf16[768,256]{1,0:T(8,128)(2,1)S(1)}, bf16[768,256]{1,0:T(8,128)(2,1)}, u32[]{:S(2)}, u32[]{:S(2)}) collective-permute-start(bf16[768,256]{1,0:T(8,128)(2,1)S(1)} %joined.1.refs_0_), channel_id=1, source_target_pairs={{0,248},{8,0},{16,8},{24,16},{32,24},{40,32},{48,40},{56,48},{64,5... | collective-permute-start | bytes 1179656 | tf_op jit(solution)/shard_map/ppermute | solution.py:229
  136.2 1.0 copy-start.2
  137.2 1.0 copy-start.3
  142.7 1.0 copy-start
  143.7 0.6 copy-start.4
  148.2 13.9 %copy-start.1 = (f32[2048,128]{1,0:T(8,128)S(1)}, f32[2048,128]{1,0:T(8,128)}, u32[]{:S(2)}) copy-start(f32[2048,128]{1,0:T(8,128)} %copy-done) | copy-start | bytes 3145732
  148.2 13.9 %all-to-all-start.1 = ((bf16[4,272,256]{2,1,0:T(8,128)(2,1)}), bf16[4,272,256]{2,1,0:T(8,128)(2,1)S(1)}, u32[]{:S(2)}, u32[]{:S(2)}) async-start(bf16[4,272,256]{2,1,0:T(8,128)(2,1)} %project.1), calls=%async_computation.1 | async-start | bytes 1114112 | tf_op jit(solution)/shard_map/all_to_all | solution.py:276
  162.1 0.8 copy-start.5
where the time goes:
time: 170 us; the launch traced here: 169 us
  blocking collectives  58.9 us (35%)
  waiting for transfers between devices  45.2 us (27%)
  starting transfers between devices  41 us (24%)
  Pallas kernels  14.4 us (8%)
  local copies, waits for them, and re-layouts  6.64 us (4%)
  other arithmetic  1.74 us (1%)
    all_to_all x1, blocking collectives, shards(): lax.all_to_all(jnp.broadcast_to(layer_half[None], (4, 64, columns)), 'far...  58.9 us
    ppermute x3, waiting for transfers between devices, along_x(): lax.ppermute(array, ('xl', 'xh'), [(at[x], at[(x + shift) % 4]) for x in...  20.5 us
    ppermute x4, starting transfers between devices, along_z(): return lax.ppermute(array, Z, [(z, (z + shift) % 32) for z in range(32)])  14.7 us
    ppermute x3, starting transfers between devices, along_x(): lax.ppermute(array, ('xl', 'xh'), [(at[x], at[(x + shift) % 4]) for x in...  10.5 us
    ppermute x1, waiting for transfers between devices, shards(): turned = lax.ppermute(tokens, ('y', 'xl', 'c'), exchange)  9.95 us
    all_to_all x1, waiting for transfers between devices, shards(): parts = lax.all_to_all(partial, 'y', 0, 0)  7.56 us
    ppermute x4, waiting for transfers between devices, along_z(): return lax.ppermute(array, Z, [(z, (z + shift) % 32) for z in range(32)])  7.18 us
    pallas_call x1, Pallas kernels, finish(): pl.pallas_call(finish_kernel, out_shape=[jax.ShapeDtypeStruct((TOKENS //...  5.78 us
  transfers between devices with their start and end apart: 11, of which 7 were waited for; matrix products, arithmetic and copies ran while one was open for 2% of the time, Pallas kernels for 3%

commit v1 on v0

--- a/solution.py
+++ b/solution.py
@@ -55,29 +55,41 @@
     )(tokens, gain)
 
 
-def join_kernel(*refs):
-    *parts, out_ref = refs
-    for k, part in enumerate(parts):
-        out_ref[256 * k : 256 * (k + 1), :] = part[...]
-
-
-def joined(*parts):
+def join_kernel(own_ref, below_ref, above_ref, up_ref, down_ref):
+    for out_ref, first, second, rows in (
+        (up_ref, above_ref, below_ref, slice(0, 128)),
+        (down_ref, below_ref, above_ref, slice(128, 256)),
+    ):
+        out_ref[:256, :] = own_ref[...]
+        out_ref[256:512, :] = first[...]
+        out_ref[512:, :] = second[rows, :]
+
+
+def joined(own, below, above):
     return pl.pallas_call(
         join_kernel,
-        out_shape=jax.ShapeDtypeStruct((256 * len(parts), 256), jnp.bfloat16),
-        compiler_params=pltpu.CompilerParams(vmem_limit_bytes=2 << 20),
+        out_shape=[jax.ShapeDtypeStruct((640, 256), jnp.bfloat16)] * 2,
+        compiler_params=pltpu.CompilerParams(vmem_limit_bytes=4 << 20),
         name="joined",
-    )(*parts)
+    )(own, below, above)
 
 
 def project_kernel(own_ref, other_ref, *refs):
-    w_refs, out_ref, layer = refs[:3], refs[3], refs[4]
+    up_ref, down_ref, below_ref, above_ref, out_ref, layer = refs
     near, core = lax.axis_index("near"), lax.axis_index("c")
     x = lax.axis_index("xh") * 2 + lax.axis_index("xl")
-    for w_ref, offsets in zip(w_refs, ((0, 5, 3), (7, 4, 2), (1, 6, 4))):
-        for k, offset in enumerate(offsets):
-            place = lax.rem(near + offset, 8)
-            layer[:, :, place] = w_ref[256 * k : 256 * (k + 1), :].reshape(2, 2, 64, 256)
+    for ref, at, offset in (
+        (down_ref, 0, 0),
+        (down_ref, 256, 5),
+        (up_ref, 256, 3),
+        (below_ref, 0, 7),
+        (below_ref, 256, 2),
+        (above_ref, 0, 1),
+        (above_ref, 256, 6),
+    ):
+        layer[:, :, lax.rem(near + offset, 8)] = ref[at : at + 256, :].reshape(2, 2, 64, 256)
+    for half, ref in enumerate((below_ref, above_ref)):
+        layer[half, :, lax.rem(near + 4, 8)] = ref[512:, :].reshape(2, 64, 256)
     for a_ref, c in ((own_ref, core), (other_ref, 1 - core)):
         for low in range(2):
             slots = [lax.rem(x + 4 - (2 * high + low), 4) for high in range(2)]
@@ -261,9 +273,9 @@
     other = lax.ppermute(own, "c", [(0, 1), (1, 0)])
     below = along_z(spread, 3)
     above = along_z(spread, 29)
-    held = joined(spread, below, above)
-    from_below = along_z(held, 1)
-    from_above = along_z(held, 31)
+    up, down = joined(spread, below, above)
+    from_below = along_z(up, 1)
+    from_above = along_z(down, 31)
     queries_flat = queries.reshape(TOKENS, SLICE)
     old_sums, old_stats = cached_part(
         lengths,
@@ -272,7 +284,7 @@
         head_value_cache.reshape(batch_rows * CACHE_SLOTS, HEAD_SIZE),
     )
     cosine, sine = turns(lengths, steps)
-    partial = project(own, other, [held, from_below, from_above])
+    partial = project(own, other, [up, down, from_below, from_above])
     parts = lax.all_to_all(partial, "y", 0, 0)
     attended, appended = finish(parts, cosine, sine, queries_flat, old_sums, old_stats)
     return (

time: 170 us -> 168 us (0.988)
  local copies, waits for them, and re-layouts: 6.64 us -> 4.15 us
    unnamed x22 -> x18, local copies, waits for them, and re-layouts: 4.55 us -> 2.06 us
where the time goes in v1:
time: 168 us; the launch traced here: 167 us
  blocking collectives  58.9 us (35%)
  waiting for transfers between devices  45.2 us (27%)
  starting transfers between devices  41.1 us (24%)
  Pallas kernels  15.5 us (9%)
  local copies, waits for them, and re-layouts  4.15 us (2%)
  other arithmetic  1.74 us (1%)
    all_to_all x1, blocking collectives, shards(): lax.all_to_all(jnp.broadcast_to(layer_half[None], (4, 64, columns)), 'far...  58.9 us
    ppermute x3, waiting for transfers between devices, along_x(): lax.ppermute(array, ('xl', 'xh'), [(at[x], at[(x + shift) % 4]) for x in...  20.5 us
    ppermute x4, starting transfers between devices, along_z(): return lax.ppermute(array, Z, [(z, (z + shift) % 32) for z in range(32)])  14.7 us
    ppermute x3, starting transfers between devices, along_x(): lax.ppermute(array, ('xl', 'xh'), [(at[x], at[(x + shift) % 4]) for x in...  10.5 us
    ppermute x1, waiting for transfers between devices, shards(): turned = lax.ppermute(tokens, ('y', 'xl', 'c'), exchange)  9.95 us
    all_to_all x1, waiting for transfers between devices, shards(): parts = lax.all_to_all(partial, 'y', 0, 0)  7.56 us
    ppermute x4, waiting for transfers between devices, along_z(): return lax.ppermute(array, Z, [(z, (z + shift) % 32) for z in range(32)])  7.18 us
    pallas_call x1, Pallas kernels, finish(): pl.pallas_call(finish_kernel, out_shape=[jax.ShapeDtypeStruct((TOKENS //...  5.78 us
  transfers between devices with their start and end apart: 11, of which 7 were waited for; matrix products, arithmetic and copies ran while one was open for 2% of the time, Pallas kernels for 3%

profile of v1, /device:TPU:34, one launch (start us, length us, event | category | flops | bytes accessed | tf_op | source)
XLA Modules:
  0.0 167.5 jit_solution(10253966129860940906)
XLA Ops:
  0.6 5.1 %collective-permute-start = (bf16[64,4,1024]{2,1,0:T(4,128)(2,1)}, bf16[64,4,1024]{2,1,0:T(4,128)(2,1)S(1)}, u32[]{:S(2)}, u32[]{:S(2)}) collective-permute-start(bf16[64,4,1024]{2,1,0:T(4,128)(2,1)} %param.10), channel_id=1, source_target_pairs={{0,0},{2,256},{4,512},{6,768},{256,2},{258,258},{260,514},{262,770... | collective-permute-start | bytes 1572872 | tf_op jit(solution)/shard_map/ppermute | solution.py:258
  5.7 0.7 reshape.53
  6.4 3.2 %collective-permute-start.1 = (bf16[1,1024]{1,0:T(2,128)(2,1)S(1)}, bf16[1,1024]{1,0:T(2,128)(2,1)S(1)}, u32[]{:S(2)}, u32[]{:S(2)}) collective-permute-start(bf16[1,1024]{1,0:T(2,128)(2,1)S(1)} %reshape.53), channel_id=1, source_target_pairs={{0,0},{2,256},{4,512},{6,768},{256,2},{258,258},{260,514},{262,770... | collective-permute-start | bytes 6152 | tf_op jit(solution)/shard_map/ppermute | solution.py:259
  9.6 10.0 %collective-permute-done = bf16[64,4,1024]{2,1,0:T(4,128)(2,1)S(1)} collective-permute-done((bf16[64,4,1024]{2,1,0:T(4,128)(2,1)}, bf16[64,4,1024]{2,1,0:T(4,128)(2,1)S(1)}, u32[]{:S(2)}, u32[]{:S(2)}) %collective-permute-start) | collective-permute-done | bytes 524320 | tf_op jit(solution)/shard_map/ppermute | solution.py:258
  19.5 0.1 reshape.52.tokens_ref
  19.6 0.0 collective-permute-done.1.gain_ref
  19.7 0.3 prepare.1
  19.9 1.9 %collective-permute-start.2 = (bf16[272,1024]{1,0:T(8,128)(2,1)S(1)}, bf16[272,1024]{1,0:T(8,128)(2,1)S(1)}, u32[]{:S(2)}, u32[]{:S(2)}) collective-permute-start(bf16[272,1024]{1,0:T(8,128)(2,1)S(1)} %prepare.1), channel_id=1, source_target_pairs={{0,4},{4,1},{1,5},{5,0},{2,6},{6,3},{3,7},{7,2},{8,12},{12,9},{9,1... | collective-permute-start | bytes 1671176 | tf_op jit(solution)/shard_map/ppermute | solution.py:237
  21.8 4.0 %collective-permute-start.3 = (bf16[272,1024]{1,0:T(8,128)(2,1)S(1)}, bf16[272,1024]{1,0:T(8,128)(2,1)S(1)}, u32[]{:S(2)}, u32[]{:S(2)}) collective-permute-start(bf16[272,1024]{1,0:T(8,128)(2,1)S(1)} %prepare.1), channel_id=1, source_target_pairs={{0,1},{4,5},{1,0},{5,4},{2,3},{6,7},{3,2},{7,6},{8,9},{12,13},{9,8... | collective-permute-start | bytes 1671176 | tf_op jit(solution)/shard_map/ppermute | solution.py:237
  25.9 4.5 %collective-permute-start.4 = (bf16[272,1024]{1,0:T(8,128)(2,1)S(1)}, bf16[272,1024]{1,0:T(8,128)(2,1)S(1)}, u32[]{:S(2)}, u32[]{:S(2)}) collective-permute-start(bf16[272,1024]{1,0:T(8,128)(2,1)S(1)} %prepare.1), channel_id=1, source_target_pairs={{0,5},{4,0},{1,4},{5,1},{2,7},{6,2},{3,6},{7,3},{8,13},{12,8},{9,1... | collective-permute-start | bytes 1671176 | tf_op jit(solution)/shard_map/ppermute | solution.py:237
  30.4 6.9 %collective-permute-done.2 = bf16[272,1024]{1,0:T(8,128)(2,1)S(1)} collective-permute-done((bf16[272,1024]{1,0:T(8,128)(2,1)S(1)}, bf16[272,1024]{1,0:T(8,128)(2,1)S(1)}, u32[]{:S(2)}, u32[]{:S(2)}) %collective-permute-start.2) | collective-permute-done | bytes 557088 | tf_op jit(solution)/shard_map/ppermute | solution.py:237
  37.3 3.5 %collective-permute-done.3 = bf16[272,1024]{1,0:T(8,128)(2,1)S(1)} collective-permute-done((bf16[272,1024]{1,0:T(8,128)(2,1)S(1)}, bf16[272,1024]{1,0:T(8,128)(2,1)S(1)}, u32[]{:S(2)}, u32[]{:S(2)}) %collective-permute-start.3) | collective-permute-done | bytes 557088 | tf_op jit(solution)/shard_map/ppermute | solution.py:237
  40.8 10.2 %collective-permute-done.4 = bf16[272,1024]{1,0:T(8,128)(2,1)S(1)} collective-permute-done((bf16[272,1024]{1,0:T(8,128)(2,1)S(1)}, bf16[272,1024]{1,0:T(8,128)(2,1)S(1)}, u32[]{:S(2)}, u32[]{:S(2)}) %collective-permute-start.4) | collective-permute-done | bytes 557088 | tf_op jit(solution)/shard_map/ppermute | solution.py:237
  51.0 0.0 copy-start.4
  51.0 0.3 pad_maximum_fusion.own_ref
  51.3 0.0 copy-start.2
  51.3 2.1 %collective-permute-start.5 = (bf16[4,272,1024]{2,1,0:T(8,128)(2,1)S(1)}, bf16[4,272,1024]{2,1,0:T(8,128)(2,1)}, u32[]{:S(2)}, u32[]{:S(2)}) collective-permute-start(bf16[4,272,1024]{2,1,0:T(8,128)(2,1)S(1)} %pad_maximum_fusion.own_ref), channel_id=1, source_target_pairs={{0,2},{2,0},{1,3},{3,1},{4,6},{6,4},{5,7},{7,5},{8,10},{10,8},{9,1... | collective-permute-start | bytes 6684680 | tf_op jit(solution)/shard_map/ppermute | solution.py:273
  53.3 0.0 copy-done.5
  53.4 0.0 copy-done.6
  53.4 0.0 copy-done.7
  53.4 0.0 copy-done.8
  53.4 0.7 fusion.2
  54.1 58.9 %all_to_all.10 = bf16[4,64,256]{2,1,0:T(8,128)(2,1)S(1)} all-to-all(bf16[4,64,256]{2,1,0:T(8,128)(2,1)S(1)} %broadcast_in_dim.2), channel_id=1, replica_groups=mesh['y'=4,'far'=4,'near'=8,'xl'=2,'c'=2,'xh'=2] {'far'}, dimensions={0} | all-to-all | bytes 262144 | tf_op jit(solution)/shard_map/all_to_all | solution.py:267
  113.0 5.1 %collective-permute-start.6 = (bf16[256,256]{1,0:T(8,128)(2,1)S(1)}, bf16[256,256]{1,0:T(8,128)(2,1)S(1)}, u32[]{:S(2)}, u32[]{:S(2)}) collective-permute-start(bf16[256,256]{1,0:T(8,128)(2,1)S(1)} %bitcast.8), channel_id=1, source_target_pairs={{0,24},{8,32},{16,40},{24,48},{32,56},{40,64},{48,72},{56,80},{64,... | collective-permute-start | bytes 393224 | tf_op jit(solution)/shard_map/ppermute | solution.py:241
  118.1 3.8 %collective-permute-start.7 = (bf16[256,256]{1,0:T(8,128)(2,1)S(1)}, bf16[256,256]{1,0:T(8,128)(2,1)S(1)}, u32[]{:S(2)}, u32[]{:S(2)}) collective-permute-start(bf16[256,256]{1,0:T(8,128)(2,1)S(1)} %bitcast.9), channel_id=1, source_target_pairs={{0,232},{8,240},{16,248},{24,0},{32,8},{40,16},{48,24},{56,32},{64... | collective-permute-start | bytes 393224 | tf_op jit(solution)/shard_map/ppermute | solution.py:241
  121.9 1.0 collective-permute-done.6.below_ref
  122.9 6.2 %collective-permute-done.7.above_ref = bf16[256,256]{1,0:T(8,128)(2,1)S(1)} collective-permute-done((bf16[256,256]{1,0:T(8,128)(2,1)S(1)}, bf16[256,256]{1,0:T(8,128)(2,1)S(1)}, u32[]{:S(2)}, u32[]{:S(2)}) %collective-permute-start.7) | collective-permute-done | bytes 131104 | tf_op jit(solution)/shard_map/ppermute | solution.py:241
  129.1 0.9 joined.1
  129.9 1.9 %collective-permute-start.8 = (bf16[640,256]{1,0:T(8,128)(2,1)}, bf16[640,256]{1,0:T(8,128)(2,1)}, u32[]{:S(2)}, u32[]{:S(2)}) collective-permute-start(bf16[640,256]{1,0:T(8,128)(2,1)} %get-tuple-element.11.refs_0_), channel_id=1, source_target_pairs={{0,8},{8,16},{16,24},{24,32},{32,40},{40,48},{48,56},{56,64},{64,7... | collective-permute-start | bytes 983048 | tf_op jit(solution)/shard_map/ppermute | solution.py:241
  131.9 3.9 %collective-permute-start.9 = (bf16[640,256]{1,0:T(8,128)(2,1)}, bf16[640,256]{1,0:T(8,128)(2,1)}, u32[]{:S(2)}, u32[]{:S(2)}) collective-permute-start(bf16[640,256]{1,0:T(8,128)(2,1)} %get-tuple-element.12.refs_1_), channel_id=1, source_target_pairs={{0,248},{8,0},{16,8},{24,16},{32,24},{40,32},{48,40},{56,48},{64,5... | collective-permute-start | bytes 983048 | tf_op jit(solution)/shard_map/ppermute | solution.py:241
  135.8 0.0 copy-done.4
  135.8 0.1 add_convert_fusion
  135.9 0.1 convert_element_type.15
  136.0 1.2 reshape.55.queries_ref
  137.2 0.0 copy-start.3
  137.2 1.0 copy-done.3
  138.2 4.5 %cached.1 = (f32[2048,128]{1,0:T(8,128)S(1)}, f32[128,128]{1,0:T(8,128)S(1)}) custom-call(s32[64]{0:T(128)S(1)} %copy-done.4, bf16[256,1024]{1,0:T(8,128)(2,1)S(1)} %reshape.55.queries_ref, bf16[2048,128]{1,0:T(8,128)(2,1)S(1)} %bitcast.11, bf16[2048,128]{1,0:T(8,128)(2,1)S(1)} %bitcast.12), custom_call_target="tpu_custom_call" | custom-call | flops 150000000 | bytes 3145728 | tf_op jit(solution)/shard_map/cached/pallas_call | solution.py:155
  142.7 1.0 copy-done
  143.7 0.0 collective-permute-done.8.refs_2_
  143.7 0.0 collective-permute-done.9.refs_3_
  143.7 0.0 collective-permute-done.5.other_ref
  143.7 4.1 %project.1 = bf16[4,272,256]{2,1,0:T(8,128)(2,1)} custom-call(bf16[4,272,1024]{2,1,0:T(8,128)(2,1)S(1)} %pad_maximum_fusion.own_ref, bf16[4,272,1024]{2,1,0:T(8,128)(2,1)} %collective-permute-done.5.other_ref, bf16[640,256]{1,0:T(8,128)(2,1)} %get-tuple-element.11.refs_0_, bf16[640,256]{1,0:T(8,128)(2,1)} %get-tuple-element.12.refs_1_, ...), custom_call_target="tpu_custom_call" | custom-call | tf_op jit(solution)/shard_map/project/pallas_call | solution.py:111
  147.8 5.7 %all-to-all-start.1 = ((bf16[4,272,256]{2,1,0:T(8,128)(2,1)}), bf16[4,272,256]{2,1,0:T(8,128)(2,1)S(1)}, u32[]{:S(2)}, u32[]{:S(2)}) async-start(bf16[4,272,256]{2,1,0:T(8,128)(2,1)} %project.1), calls=%async_computation.1 | async-start | bytes 1114112 | tf_op jit(solution)/shard_map/all_to_all | solution.py:288
  153.5 0.5 fusion.1
  154.0 0.1 pad_maximum_fusion.1
  154.1 7.6 %all-to-all-done.1.parts_ref = bf16[4,272,256]{2,1,0:T(8,128)(2,1)S(1)} async-done(((bf16[4,272,256]{2,1,0:T(8,128)(2,1)}), bf16[4,272,256]{2,1,0:T(8,128)(2,1)S(1)}, u32[]{:S(2)}, u32[]{:S(2)}) %all-to-all-start.1) | async-done | bytes 557088 | tf_op jit(solution)/shard_map/all_to_all | solution.py:288
  161.7 0.0 copy-done.1
  161.7 5.8 %finish.1 = (bf16[64,4,1024]{2,1,0:T(4,128)(2,1)}, bf16[64,4,256]{2,1,0:T(4,128)(2,1)}) custom-call(bf16[4,272,256]{2,1,0:T(8,128)(2,1)S(1)} %all-to-all-done.1.parts_ref, f32[256,128]{1,0:T(8,128)S(1)} %get-tuple-element.24.cosine_ref, f32[256,128]{1,0:T(8,128)S(1)} %get-tuple-element.25.sine_ref, bf16[256,1024]{1,0:T(8,128)(2,1)S(1)} %reshape.55.queries_ref, ...), custom_call_target="tpu_custom_call" | custom-call | tf_op jit(solution)/shard_map/finish/pallas_call | solution.py:215
  (9 shorter events, 0.0 us)
Async XLA Ops:
  0.6 18.9 %collective-permute-start = (bf16[64,4,1024]{2,1,0:T(4,128)(2,1)}, bf16[64,4,1024]{2,1,0:T(4,128)(2,1)S(1)}, u32[]{:S(2)}, u32[]{:S(2)}) collective-permute-start(bf16[64,4,1024]{2,1,0:T(4,128)(2,1)} %param.10), channel_id=1, source_target_pairs={{0,0},{2,256},{4,512},{6,768},{256,2},{258,258},{260,514},{262,770... | collective-permute-start | bytes 1572872 | tf_op jit(solution)/shard_map/ppermute | solution.py:258
  6.4 13.2 %collective-permute-start.1 = (bf16[1,1024]{1,0:T(2,128)(2,1)S(1)}, bf16[1,1024]{1,0:T(2,128)(2,1)S(1)}, u32[]{:S(2)}, u32[]{:S(2)}) collective-permute-start(bf16[1,1024]{1,0:T(2,128)(2,1)S(1)} %reshape.53), channel_id=1, source_target_pairs={{0,0},{2,256},{4,512},{6,768},{256,2},{258,258},{260,514},{262,770... | collective-permute-start | bytes 6152 | tf_op jit(solution)/shard_map/ppermute | solution.py:259
  19.9 17.4 %collective-permute-start.2 = (bf16[272,1024]{1,0:T(8,128)(2,1)S(1)}, bf16[272,1024]{1,0:T(8,128)(2,1)S(1)}, u32[]{:S(2)}, u32[]{:S(2)}) collective-permute-start(bf16[272,1024]{1,0:T(8,128)(2,1)S(1)} %prepare.1), channel_id=1, source_target_pairs={{0,4},{4,1},{1,5},{5,0},{2,6},{6,3},{3,7},{7,2},{8,12},{12,9},{9,1... | collective-permute-start | bytes 1671176 | tf_op jit(solution)/shard_map/ppermute | solution.py:237
  21.8 18.9 %collective-permute-start.3 = (bf16[272,1024]{1,0:T(8,128)(2,1)S(1)}, bf16[272,1024]{1,0:T(8,128)(2,1)S(1)}, u32[]{:S(2)}, u32[]{:S(2)}) collective-permute-start(bf16[272,1024]{1,0:T(8,128)(2,1)S(1)} %prepare.1), channel_id=1, source_target_pairs={{0,1},{4,5},{1,0},{5,4},{2,3},{6,7},{3,2},{7,6},{8,9},{12,13},{9,8... | collective-permute-start | bytes 1671176 | tf_op jit(solution)/shard_map/ppermute | solution.py:237
  25.9 25.1 %collective-permute-start.4 = (bf16[272,1024]{1,0:T(8,128)(2,1)S(1)}, bf16[272,1024]{1,0:T(8,128)(2,1)S(1)}, u32[]{:S(2)}, u32[]{:S(2)}) collective-permute-start(bf16[272,1024]{1,0:T(8,128)(2,1)S(1)} %prepare.1), channel_id=1, source_target_pairs={{0,5},{4,0},{1,4},{5,1},{2,7},{6,2},{3,6},{7,3},{8,13},{12,8},{9,1... | collective-permute-start | bytes 1671176 | tf_op jit(solution)/shard_map/ppermute | solution.py:237
  51.0 2.4 %copy-start.5 = (f32[64,256]{1,0:T(8,128)S(1)}, f32[64,256]{1,0:T(8,128)}, u32[]{:S(2)}) copy-start(f32[64,256]{1,0:T(8,128)} %param.16) | copy-start | bytes 196612
  51.0 2.4 %copy-start.6 = (f32[64,256]{1,0:T(8,128)S(1)}, f32[64,256]{1,0:T(8,128)}, u32[]{:S(2)}) copy-start(f32[64,256]{1,0:T(8,128)} %param.19) | copy-start | bytes 196612
  51.0 2.4 %copy-start.7 = (f32[64,256]{1,0:T(8,128)S(1)}, f32[64,256]{1,0:T(8,128)}, u32[]{:S(2)}) copy-start(f32[64,256]{1,0:T(8,128)} %param.17) | copy-start | bytes 196612
  51.0 2.4 %copy-start.8 = (f32[64,256]{1,0:T(8,128)S(1)}, f32[64,256]{1,0:T(8,128)}, u32[]{:S(2)}) copy-start(f32[64,256]{1,0:T(8,128)} %param.18) | copy-start | bytes 196612
  51.0 84.8 %copy-start.4 = (s32[64]{0:T(128)S(1)}, s32[64]{0:T(128)}, u32[]{:S(2)}) copy-start(s32[64]{0:T(128)} %lengths_ref.1) | copy-start | bytes 772
  51.3 85.9 %copy-start.2 = (bf16[64,32,128]{2,1,0:T(8,128)(2,1)S(1)}, bf16[64,32,128]{2,1,0:T(8,128)(2,1)}, u32[]{:S(2)}) copy-start(bf16[64,32,128]{2,1,0:T(8,128)(2,1)} %param.13) | copy-start | bytes 1572868
  51.3 92.4 %collective-permute-start.5 = (bf16[4,272,1024]{2,1,0:T(8,128)(2,1)S(1)}, bf16[4,272,1024]{2,1,0:T(8,128)(2,1)}, u32[]{:S(2)}, u32[]{:S(2)}) collective-permute-start(bf16[4,272,1024]{2,1,0:T(8,128)(2,1)S(1)} %pad_maximum_fusion.own_ref), channel_id=1, source_target_pairs={{0,2},{2,0},{1,3},{3,1},{4,6},{6,4},{5,7},{7,5},{8,10},{10,8},{9,1... | collective-permute-start | bytes 6684680 | tf_op jit(solution)/shard_map/ppermute | solution.py:273
  113.0 9.9 %collective-permute-start.6 = (bf16[256,256]{1,0:T(8,128)(2,1)S(1)}, bf16[256,256]{1,0:T(8,128)(2,1)S(1)}, u32[]{:S(2)}, u32[]{:S(2)}) collective-permute-start(bf16[256,256]{1,0:T(8,128)(2,1)S(1)} %bitcast.8), channel_id=1, source_target_pairs={{0,24},{8,32},{16,40},{24,48},{32,56},{40,64},{48,72},{56,80},{64,... | collective-permute-start | bytes 393224 | tf_op jit(solution)/shard_map/ppermute | solution.py:241
  118.1 11.0 %collective-permute-start.7 = (bf16[256,256]{1,0:T(8,128)(2,1)S(1)}, bf16[256,256]{1,0:T(8,128)(2,1)S(1)}, u32[]{:S(2)}, u32[]{:S(2)}) collective-permute-start(bf16[256,256]{1,0:T(8,128)(2,1)S(1)} %bitcast.9), channel_id=1, source_target_pairs={{0,232},{8,240},{16,248},{24,0},{32,8},{40,16},{48,24},{56,32},{64... | collective-permute-start | bytes 393224 | tf_op jit(solution)/shard_map/ppermute | solution.py:241
  129.9 13.8 %collective-permute-start.8 = (bf16[640,256]{1,0:T(8,128)(2,1)}, bf16[640,256]{1,0:T(8,128)(2,1)}, u32[]{:S(2)}, u32[]{:S(2)}) collective-permute-start(bf16[640,256]{1,0:T(8,128)(2,1)} %get-tuple-element.11.refs_0_), channel_id=1, source_target_pairs={{0,8},{8,16},{16,24},{24,32},{32,40},{40,48},{48,56},{56,64},{64,7... | collective-permute-start | bytes 983048 | tf_op jit(solution)/shard_map/ppermute | solution.py:241
  131.9 11.8 %collective-permute-start.9 = (bf16[640,256]{1,0:T(8,128)(2,1)}, bf16[640,256]{1,0:T(8,128)(2,1)}, u32[]{:S(2)}, u32[]{:S(2)}) collective-permute-start(bf16[640,256]{1,0:T(8,128)(2,1)} %get-tuple-element.12.refs_1_), channel_id=1, source_target_pairs={{0,248},{8,0},{16,8},{24,16},{32,24},{40,32},{48,40},{56,48},{64,5... | collective-permute-start | bytes 983048 | tf_op jit(solution)/shard_map/ppermute | solution.py:241
  137.2 1.0 copy-start.3
  142.7 1.0 copy-start
  147.8 13.9 %copy-start.1 = (f32[2048,128]{1,0:T(8,128)S(1)}, f32[2048,128]{1,0:T(8,128)}, u32[]{:S(2)}) copy-start(f32[2048,128]{1,0:T(8,128)} %copy-done) | copy-start | bytes 3145732
  147.8 13.9 %all-to-all-start.1 = ((bf16[4,272,256]{2,1,0:T(8,128)(2,1)}), bf16[4,272,256]{2,1,0:T(8,128)(2,1)S(1)}, u32[]{:S(2)}, u32[]{:S(2)}) async-start(bf16[4,272,256]{2,1,0:T(8,128)(2,1)} %project.1), calls=%async_computation.1 | async-start | bytes 1114112 | tf_op jit(solution)/shard_map/all_to_all | solution.py:288
